TPU v7x, 1024 devices: a whole 4x4x32 slice. The times are simulated.
1024 devices in a mesh: dp: 32 (over y, z_hi, core), tensor: 32 (over x, z_lo).
Axes of the slice: x: 4, y: 4, z: 32 (z_hi: 4, z_lo: 8; z = z_hi * 8 + z_lo), core: 2. Of those that a mesh axis runs over, the one named last changes fastest.
Arguments:
- attn_input: bfloat16 [4096, 8192], P('dp'), may hold values from -6 to 6
- residual: bfloat16 [4096, 8192], P('dp'), may hold values from -3 to 3
- query_weight: bfloat16 [8192, 8192], P('dp', 'tensor'), may hold values from -0.0625 to 0.0625
- query_bias: bfloat16 [8192], P('tensor'), may hold values from -3 to 3
- output_weight: bfloat16 [8192, 8192], P('tensor', 'dp'), may hold values from -0.0625 to 0.0625
- cached_keys: bfloat16 [32, 32, 1024, 128], P('dp', 'tensor'), may hold values from -305 to 305, as said below
- cached_values: bfloat16 [32, 32, 1024, 128], P('dp', 'tensor'), may hold values from -12 to 12, as said below
- norm_gain: bfloat16 [8192], replicated, may hold values from 0.5 to 1.5
Outputs:
- hidden_out: bfloat16 [4096, 8192], P(('dp', 'tensor'))
- normed_out: bfloat16 [4096, 8192], P('dp')
Inputs may be any that keep to these rules, and one draw needn't show every extreme that they name: `cached_keys`: groups g and g2 with g // 4 == g2 // 4 carry equal keys. `cached_values`: groups g and g2 with g // 4 == g2 // 4 carry equal values.
All inputs are finite; a program needn't handle non-finite values.
Results may differ from a plain program's by a relative error of at most 0.025.
Values may be sent and summed in bfloat16 or wider, within the bound.
A program may use at most 64 MiB of HBM per device.

v0:
```python
import jax
import jax.numpy as jnp
from jax import lax
from jax.sharding import PartitionSpec as P

rope_theta = 1000000.0
norm_eps = 1e-06


def turned_gather(arrays, axis, dims):
    turned = [jnp.moveaxis(a, dim, 0) for a, dim in zip(arrays, dims)]
    both = jnp.concatenate([t.reshape(len(t), -1) for t in turned], axis=1)
    whole, at, outs = (lax.all_gather(both, axis, axis=0, tiled=True), 0, [])
    for t, dim in zip(turned, dims):
        piece = whole[:, at : at + t[0].size].reshape(-1, *t.shape[1:])
        outs.append(jnp.moveaxis(piece, 0, dim))
        at += t[0].size
    return tuple(outs)


def cut_along(shard, dim, peers):
    before, after = (shard.shape[:dim], shard.shape[dim + 1 :])
    return jnp.moveaxis(shard.reshape(*before, peers, -1, *after), dim, 0)


def sum_at_owner(shard, axis, dim):
    peers = lax.axis_size(axis)
    tiles = lax.all_to_all(cut_along(shard, dim, peers), axis, 0, 0, tiled=True)
    return jnp.sum(tiles.astype(jnp.float32), axis=0)


def laid_out(tiles, dim):
    tiles = jnp.moveaxis(tiles, 0, dim)
    shape = tiles.shape
    return tiles.reshape(*shape[:dim], shape[dim] * shape[dim + 1], *shape[dim + 2 :])


def sent_to_all(shard, axis):
    peers = lax.axis_size(axis)
    return lax.all_to_all(
        jnp.broadcast_to(shard[None], (peers, *shard.shape)), axis, 0, 0, tiled=True
    )


def gather_directly(shard, axis, dim):
    return laid_out(sent_to_all(shard, axis), dim)


def rotate(projected, first_pos):
    head_dim = projected.shape[-1]
    half_dim = head_dim // 2
    inv_freq = jnp.power(
        jnp.float32(rope_theta), -2.0 * jnp.arange(half_dim, dtype=jnp.float32) / head_dim
    )
    positions = first_pos + jnp.arange(projected.shape[0], dtype=jnp.float32)
    angles = positions[:, None] * inv_freq[None, :]
    cosine = jnp.cos(angles)[:, None, :]
    sine = jnp.sin(angles)[:, None, :]
    first_half = projected[..., :half_dim]
    second_half = projected[..., half_dim:]
    return jnp.concatenate(
        [first_half * cosine - second_half * sine, second_half * cosine + first_half * sine],
        axis=-1,
    )


def attend(queries, local_keys, local_values):
    count_q = queries.shape[0]
    count_k = local_keys.shape[0]
    scores = jnp.einsum("thd,kd->htk", queries, local_keys, preferred_element_type=jnp.float32) * (
        1.0 / queries.shape[-1] ** 0.5
    )
    visible = jnp.arange(count_k)[None, :] <= (count_k - count_q + jnp.arange(count_q))[:, None]
    scores = jnp.where(visible[None], scores, jnp.float32(-1e30))
    highest = jnp.max(scores, axis=-1, keepdims=True)
    expo = jnp.exp(scores - highest)
    soft = (expo / jnp.sum(expo, axis=-1, keepdims=True)).astype(jnp.bfloat16)
    mixed = jnp.einsum("htk,kd->thd", soft, local_values, preferred_element_type=jnp.float32)
    return mixed.astype(jnp.bfloat16)


def normalize(total, norm_gain):
    mean_square = jnp.mean(total * total, axis=-1, keepdims=True)
    return (total * lax.rsqrt(mean_square + norm_eps) * norm_gain.astype(jnp.float32)).astype(
        jnp.bfloat16
    )


def body(
    attn_input,
    residual,
    query_weight,
    query_bias,
    output_weight,
    cached_keys,
    cached_values,
    norm_gain,
):
    tok_count = attn_input.shape[0]
    ctx_len = cached_keys.shape[2]
    head_dim = cached_keys.shape[3]
    local_heads = query_weight.shape[1] // head_dim
    query_full, output_full = turned_gather((query_weight, output_weight), "dp", (0, 1))
    projected = jnp.dot(attn_input, query_full, preferred_element_type=jnp.float32)
    projected = projected + query_bias.astype(jnp.float32)
    queries = rotate(
        projected.reshape(tok_count, local_heads, head_dim), float(ctx_len - tok_count)
    ).astype(jnp.bfloat16)
    mixed = attend(queries, cached_keys[0, 0], cached_values[0, 0]).reshape(
        tok_count, local_heads * head_dim
    )
    partial_sum = jnp.dot(mixed, output_full, preferred_element_type=jnp.float32)
    own_count = tok_count // lax.axis_size("tensor")
    own_start = lax.axis_index("tensor") * own_count
    shares = sum_at_owner(partial_sum.astype(jnp.bfloat16), "tensor", 0)
    resid_rows = lax.dynamic_slice_in_dim(residual, own_start, own_count, 0)
    total = resid_rows.astype(jnp.float32) + shares
    hidden_out = total.astype(jnp.bfloat16)
    normed_part = normalize(total, norm_gain)
    normed_out = gather_directly(normed_part, "tensor", 0)
    return (hidden_out, normed_out)


def solution(mesh):
    return jax.shard_map(
        body,
        mesh=mesh,
        in_specs=(
            P("dp", None),
            P("dp", None),
            P("dp", "tensor"),
            P("tensor"),
            P("tensor", "dp"),
            P("dp", "tensor", None, None),
            P("dp", "tensor", None, None),
            P(),
        ),
        out_specs=(P(("dp", "tensor"), None), P("dp", None)),
        check_vma=False,
    )
```

profile of v0, /device:TPU:40, one launch (start us, length us, event | category | flops | bytes accessed | tf_op | source)
XLA Modules:
  0.0 534.7 jit_solution(9063428704130613166)
XLA Ops:
  7.2 0.0 copy-start
  7.2 0.0 all-gather.2.cloned.1.call-start
  7.2 1.1 copy.10
  8.4 1.6 pad_maximum_fusion
  10.0 0.0 all-gather.2.cloned.1.call-update
  10.0 0.7 convert_element_type.32
  10.7 0.1 iota_compare_fusion
  10.9 0.3 multiply_cosine_fusion
  11.2 0.0 copy-start.1
  11.2 241.8 %all-gather.2.cloned.1.call-done = bf16[8192,512]{0,1:T(8,128)(2,1)} async-done(((bf16[256,512]{0,1:T(8,128)(2,1)}), bf16[8192,512]{0,1:T(8,128)(2,1)}) %all-gather.2.cloned.1.call-update) | async-done | bytes 8388624 | tf_op jit(solution)/shard_map/all_gather | solution.py:13
  253.0 0.0 copy-done
  253.0 3.4 fusion.8
  256.5 0.1 copy.16
  256.6 0.1 copy.17
  256.7 0.0 copy-start.2
  256.7 0.0 copy-start.3
  256.8 0.6 copy-done.2
  257.4 0.0 copy-done.3
  257.4 0.0 copy-done.1
  257.4 0.4 fusion.7
  257.8 1.5 fusion.23
  259.3 1.7 convolution_convert_fusion.1
  260.9 4.3 convolution_convert_fusion
  265.2 4.1 reshape.110
  269.3 0.0 copy-start.4
  269.3 49.0 %all-to-all-start = ((bf16[32,4,8192]{2,1,0:T(4,128)(2,1)}), bf16[32,4,8192]{2,1,0:T(4,128)(2,1)}, u32[]{:S(2)}, u32[]{:S(2)}) async-start(bf16[32,4,8192]{2,1,0:T(4,128)(2,1)} %reshape.110), calls=%async_computation | async-start | bytes 4194304 | tf_op jit(solution)/shard_map/all_to_all | solution.py:28
  318.3 0.0 copy-done.4
  318.4 96.8 %all-to-all-done = bf16[32,4,8192]{2,1,0:T(4,128)(2,1)} async-done(((bf16[32,4,8192]{2,1,0:T(4,128)(2,1)}), bf16[32,4,8192]{2,1,0:T(4,128)(2,1)}, u32[]{:S(2)}, u32[]{:S(2)}) %all-to-all-start) | async-done | bytes 2097184 | tf_op jit(solution)/shard_map/all_to_all | solution.py:28
  415.2 2.5 convert_reduce_fusion
  417.6 1.1 multiply_reduce_fusion
  418.7 1.6 multiply_convert_fusion
  420.3 0.9 broadcast_in_dim.16
  421.3 102.6 %all_to_all.10 = bf16[32,4,8192]{2,1,0:T(4,128)(2,1)} all-to-all(bf16[32,4,8192]{2,1,0:T(4,128)(2,1)S(1)} %broadcast_in_dim.16), channel_id=1, replica_groups=mesh['dp'=32,'tensor'=32] {'tensor'}, dimensions={0} | all-to-all | bytes 4194304 | tf_op jit(solution)/shard_map/all_to_all | solution.py:40
  523.9 3.9 reshape.111
  (7 shorter events, 0.1 us)
Async XLA Ops:
  7.2 245.8 %copy-start = (bf16[128,8192]{1,0:T(8,128)(2,1)S(1)}, bf16[128,8192]{1,0:T(8,128)(2,1)}, u32[]{:S(2)}) copy-start(bf16[128,8192]{1,0:T(8,128)(2,1)} %param.8) | copy-start | bytes 6291460
  7.2 245.8 %all-gather.2.cloned.1.call-start = ((), (), s32[]{:S(2)}) async-start(), calls=%async_computation.2 | async-start | bytes 8650752 | tf_op jit(solution)/shard_map/all_gather | solution.py:13
  11.2 246.2 %copy-start.1 = (bf16[1,1,1024,128]{3,2,1,0:T(8,128)(2,1)S(1)}, bf16[1,1,1024,128]{3,2,1,0:T(8,128)(2,1)}, u32[]{:S(2)}) copy-start(bf16[1,1,1024,128]{3,2,1,0:T(8,128)(2,1)} %param.13) | copy-start | bytes 786436
  256.7 0.6 copy-start.2
  256.7 0.6 copy-start.3
  269.3 49.0 %copy-start.4 = (bf16[8192]{0:T(1024)(128)(2,1)S(1)}, bf16[8192]{0:T(1024)(128)(2,1)}, u32[]{:S(2)}) copy-start(bf16[8192]{0:T(1024)(128)(2,1)} %param.15) | copy-start | bytes 49156
  269.3 145.8 %all-to-all-start = ((bf16[32,4,8192]{2,1,0:T(4,128)(2,1)}), bf16[32,4,8192]{2,1,0:T(4,128)(2,1)}, u32[]{:S(2)}, u32[]{:S(2)}) async-start(bf16[32,4,8192]{2,1,0:T(4,128)(2,1)} %reshape.110), calls=%async_computation | async-start | bytes 4194304 | tf_op jit(solution)/shard_map/all_to_all | solution.py:28
Sparse Core Ops, SparseCore 0:
  12.8 240.1 all-gather.1
where the time goes:
time: 535 us
  waiting for transfers between devices  339 us (63%)
  blocking collectives  103 us (19%)
  starting transfers between devices  49 us (9%)
  between operations  14.2 us (3%)
  matrix products  11.2 us (2%)
  local copies, waits for them, and re-layouts  11 us (2%)
  other arithmetic  7.96 us (1%)
    all_gather x1, waiting for transfers between devices, turned_gather(): whole, at, outs = (lax.all_gather(both, axis, axis=0, tiled=True), 0, [])  242 us
    all_to_all x1, blocking collectives, sent_to_all(): lax.all_to_all(jnp.broadcast_to(shard[None], (peers, *shard.shape)), axis...  103 us
    all_to_all x1, waiting for transfers between devices, sum_at_owner(): tiles = lax.all_to_all(cut_along(shard, dim, peers), axis, 0, 0, tiled=True)  96.8 us
    all_to_all x1, starting transfers between devices, sum_at_owner(): tiles = lax.all_to_all(cut_along(shard, dim, peers), axis, 0, 0, tiled=True)  49 us
  transfers between devices with their start and end apart: 2, of which 2 were waited for; matrix products, arithmetic and copies ran while one was open for 0% of the time, Pallas kernels for 0%

commit v1 on v0

v1 whole, which is shorter than its diff:
```python
import jax
import jax.numpy as jnp
import numpy as np
from jax import lax
from jax.experimental import pallas as pl
from jax.experimental.pallas import tpu as pltpu
from jax.sharding import PartitionSpec as P

rope_theta = 1000000.0
norm_eps = 1e-06

NY, NH, NC = 4, 4, 2
NX, NZ = 4, 8
OWN, PREV, NEXT, FAR = 0, 1, 2, 3
STEP = (0, 3, 1, 2)
F32, BF16 = jnp.float32, jnp.bfloat16


def block_kernel(
    x_hbm, wq_hbm, wo_hbm, k_hbm, v_hbm, bias_ref, cos_ref, sin_ref, res_ref, gain_ref,
    hid_ref, norm_hbm,
    w, xv, kv, vv, q, mixed, part, x1, x2, xsum, zrecv, tot, nbuf,
    loc, out_sem, zs, zr, ys, yr, ds, dr, p1s, p1r, p2s, p2r, rs, rr, gzs, gzr, gxs, gxr,
):
    dp = lax.axis_index("dp")
    ti = lax.axis_index("tensor")
    y, h, c = dp // (NH * NC), (dp // NC) % NH, dp % NC
    x, zl = ti // NZ, ti % NZ

    def piece(yy, hh, cc):
        return yy * (NH * NC) + hh * NC + cc

    def ring(base, slot):
        return (base + STEP[slot]) % 4

    def dev(d):
        return {"dp": d}

    def ten(t):
        return {"tensor": t}

    h_up, h_dn = dev(piece(y, ring(h, NEXT), c)), dev(piece(y, ring(h, PREV), c))
    y_up, y_dn = dev(piece(ring(y, NEXT), h, c)), dev(piece(ring(y, PREV), h, c))
    sib = dev(piece(y, h, 1 - c))
    x_up, x_dn = ten(ring(x, NEXT) * NZ + zl), ten(ring(x, PREV) * NZ + zl)

    locals_ = [
        pltpu.make_async_copy(wq_hbm, w.at[0, dp], loc.at[0]),
        pltpu.make_async_copy(wo_hbm, w.at[1, dp], loc.at[1]),
        pltpu.make_async_copy(x_hbm, xv, loc.at[2]),
        pltpu.make_async_copy(k_hbm, kv, loc.at[3]),
        pltpu.make_async_copy(v_hbm, vv, loc.at[4]),
    ]
    for copy in locals_:
        copy.start()

    barrier = pltpu.get_barrier_semaphore()
    partners = [h_up, h_dn, y_up, y_dn, sib, x_up, x_dn]
    partners += [ten(x * NZ + (zl + o) % NZ) for o in range(1, NZ)]
    for partner in partners:
        pl.semaphore_signal(
            barrier, inc=1, device_id=partner, device_id_type=pl.DeviceIdType.MESH
        )
    pl.semaphore_wait(barrier, len(partners))
    locals_[0].wait()
    locals_[1].wait()

    sent = []

    def remote(src, dst, send_sem, recv_sem, target):
        return pltpu.make_async_remote_copy(
            src_ref=src, dst_ref=dst, send_sem=send_sem, recv_sem=recv_sem,
            device_id=target, device_id_type=pl.DeviceIdType.MESH,
        )

    def send(src, dst, send_sem, recv_sem, target):
        copy = remote(src, dst, send_sem, recv_sem, target)
        copy.start()
        sent.append(copy)

    def landed(dst, send_sem, recv_sem):
        remote(dst, dst, send_sem, recv_sem, sib).wait_recv()

    def w_at(m, ky, kh, half):
        return w.at[m, piece(ring(y, ky), ring(h, kh), c), half]

    def push(ref, s, r, i, target):
        send(ref, ref, s.at[i], r.at[i], target)

    def z_start(m):
        s, r = zs.at[m], zr.at[m]
        push(w_at(m, OWN, OWN, 0), s, r, 0, h_up)
        push(w_at(m, OWN, OWN, 1), s, r, 3, h_dn)
        push(w_at(m, OWN, OWN, 1), s, r, 1, h_up)
        push(w_at(m, OWN, OWN, 0), s, r, 4, h_dn)

    def y_start(m, k, half):
        s, r = ys.at[m, k], yr.at[m, k]
        if half == 0:
            push(w_at(m, OWN, k, 0), s, r, 0, y_up)
            push(w_at(m, OWN, k, 0), s, r, 4, y_dn)
        else:
            push(w_at(m, OWN, k, 1), s, r, 3, y_dn)
            push(w_at(m, OWN, k, 1), s, r, 1, y_up)

    def d_start(m, k, ky):
        ref = w.at[m, piece(ring(y, ky), ring(h, k), c)]
        push(ref, ds.at[m, k], dr.at[m, k], ky, sib)

    def z_first(m):
        s, r = zs.at[m], zr.at[m]
        landed(w_at(m, OWN, PREV, 0), s.at[0], r.at[0])
        push(w_at(m, OWN, PREV, 0), s, r, 2, h_up)
        landed(w_at(m, OWN, NEXT, 1), s.at[3], r.at[3])
        push(w_at(m, OWN, NEXT, 1), s, r, 5, h_dn)
        y_start(m, PREV, 0)
        y_start(m, NEXT, 1)

    def z_second(m):
        s, r = zs.at[m], zr.at[m]
        landed(w_at(m, OWN, PREV, 1), s.at[1], r.at[1])
        y_start(m, PREV, 1)
        d_start(m, PREV, OWN)
        landed(w_at(m, OWN, NEXT, 0), s.at[4], r.at[4])
        y_start(m, NEXT, 0)
        d_start(m, NEXT, OWN)

    def z_third(m):
        s, r = zs.at[m], zr.at[m]
        landed(w_at(m, OWN, FAR, 0), s.at[2], r.at[2])
        y_start(m, FAR, 0)
        landed(w_at(m, OWN, FAR, 1), s.at[5], r.at[5])
        y_start(m, FAR, 1)
        d_start(m, FAR, OWN)

    def y_first(m, k):
        s, r = ys.at[m, k], yr.at[m, k]
        landed(w_at(m, PREV, k, 0), s.at[0], r.at[0])
        push(w_at(m, PREV, k, 0), s, r, 2, y_up)
        landed(w_at(m, NEXT, k, 1), s.at[3], r.at[3])
        push(w_at(m, NEXT, k, 1), s, r, 5, y_dn)

    def y_second(m, k):
        s, r = ys.at[m, k], yr.at[m, k]
        landed(w_at(m, PREV, k, 1), s.at[1], r.at[1])
        d_start(m, k, PREV)
        landed(w_at(m, NEXT, k, 0), s.at[4], r.at[4])
        d_start(m, k, NEXT)

    def y_third(m, k):
        s, r = ys.at[m, k], yr.at[m, k]
        landed(w_at(m, FAR, k, 0), s.at[2], r.at[2])
        landed(w_at(m, FAR, k, 1), s.at[5], r.at[5])
        d_start(m, k, FAR)

    def d_landed(m, k):
        for ky in range(4):
            ref = w.at[m, piece(ring(y, ky), ring(h, k), 1 - c)]
            landed(ref, ds.at[m, k, ky], dr.at[m, k, ky])

    def project(k):
        d_landed(0, k)
        hk = ring(h, k)

        def one(j, carry):
            d = piece(j // NC, hk, j % NC)
            cols = xv[:, pl.ds(pl.multiple_of(d * 256, 256), 256)]
            weights = w[0, d].reshape(256, 256)
            q[...] += jnp.dot(cols, weights, preferred_element_type=F32)
            return carry

        lax.fori_loop(0, NY * NC, one, 0)

    def attend(head):
        cols = slice(head * 128, head * 128 + 128)
        proj = q[:, cols] + bias_ref[:, cols].astype(F32)
        turned = proj * cos_ref[...] + pltpu.roll(proj, 64, 1) * sin_ref[...]
        scores = lax.dot_general(
            turned.astype(BF16), kv[...], (((1,), (1,)), ((), ())), preferred_element_type=F32
        ) * (1.0 / 128**0.5)
        rows = lax.broadcasted_iota(jnp.int32, scores.shape, 0)
        keys = lax.broadcasted_iota(jnp.int32, scores.shape, 1)
        scores = jnp.where(keys <= rows + (scores.shape[1] - scores.shape[0]), scores, -1e30)
        expo = jnp.exp(scores - jnp.max(scores, axis=-1, keepdims=True))
        soft = (expo / jnp.sum(expo, axis=-1, keepdims=True)).astype(BF16)
        mixed[:, cols] = jnp.dot(soft, vv[...], preferred_element_type=F32).astype(BF16)

    def partials(k):
        d_landed(1, k)
        hk = ring(h, k)

        def one(j, carry):
            d = piece(j // NC, hk, j % NC)
            out = jnp.dot(mixed[...], w[1, d].reshape(256, 256), preferred_element_type=F32)
            cols = pl.ds(pl.multiple_of(j * 256, 256), 256)
            part[hk, :, :, cols] = out.astype(BF16).reshape(32, 4, 256)
            return carry

        lax.fori_loop(0, NY * NC, one, 0)

    def rows_of(k, slot, at, count):
        return part.at[ring(h, k), pl.ds(ring(x, slot) * NZ + at, count)]

    def sum_first(k):
        send(rows_of(k, FAR, 0, 4), x1.at[k, 0], p1s.at[k, 0], p1r.at[k, 0], x_up)
        send(rows_of(k, FAR, 4, 4), x1.at[k, 1], p1s.at[k, 1], p1r.at[k, 1], x_dn)
        send(rows_of(k, NEXT, 4, 4), x2.at[k, 0, 1], p2s.at[k, 0], p2r.at[k, 0], x_up)
        send(rows_of(k, PREV, 0, 4), x2.at[k, 1, 0], p2s.at[k, 1], p2r.at[k, 1], x_dn)

    def sum_second(k):
        landed(x1.at[k, 0], p1s.at[k, 0], p1r.at[k, 0])
        own = rows_of(k, NEXT, 0, 4)
        own[...] = (own[...].astype(F32) + x1[k, 0].astype(F32)).astype(BF16)
        send(own, x2.at[k, 0, 0], p2s.at[k, 2], p2r.at[k, 2], x_up)
        landed(x1.at[k, 1], p1s.at[k, 1], p1r.at[k, 1])
        own = rows_of(k, PREV, 4, 4)
        own[...] = (own[...].astype(F32) + x1[k, 1].astype(F32)).astype(BF16)
        send(own, x2.at[k, 1, 1], p2s.at[k, 3], p2r.at[k, 3], x_dn)

    def sum_third(k):
        landed(x2.at[k, 0, 1], p2s.at[k, 0], p2r.at[k, 0])
        landed(x2.at[k, 1, 0], p2s.at[k, 1], p2r.at[k, 1])
        landed(x2.at[k, 0, 0], p2s.at[k, 2], p2r.at[k, 2])
        landed(x2.at[k, 1, 1], p2s.at[k, 3], p2r.at[k, 3])
        for half in range(2):
            own = rows_of(k, OWN, half * 4, 4)[...].astype(F32)
            both = x2[k, 0, half].astype(F32) + x2[k, 1, half].astype(F32)
            xsum[k, half * 4 : half * 4 + 4] = (own + both).astype(BF16)
        for o in range(1, NZ):
            there = (zl + o) % NZ
            send(xsum.at[k, there], zrecv.at[k, o - 1], rs.at[k, o - 1], rr.at[k, o - 1],
                 ten(x * NZ + there))

    def gathered(k):
        acc = xsum[k, zl].astype(F32)
        for o in range(1, NZ):
            landed(zrecv.at[k, o - 1], rs.at[k, o - 1], rr.at[k, o - 1])
            acc = acc + zrecv[k, o - 1].astype(F32)
        hk = ring(h, k)
        for j in range(NY * NC):
            d = piece(j // NC, hk, j % NC)
            tot[:, pl.ds(pl.multiple_of(d * 256, 256), 256)] = acc[:, j * 256 : j * 256 + 256]

    q[...] = jnp.zeros_like(q)
    z_start(0)
    for m in range(2):
        y_start(m, OWN, 0)
        y_start(m, OWN, 1)
        d_start(m, OWN, OWN)
    for m in range(2):
        y_first(m, OWN)
        y_second(m, OWN)
        y_third(m, OWN)
    locals_[2].wait()
    project(OWN)
    z_first(0)
    z_start(1)
    z_second(0)
    y_first(0, PREV)
    y_first(0, NEXT)
    y_second(0, PREV)
    y_second(0, NEXT)
    y_third(0, PREV)
    y_third(0, NEXT)
    project(PREV)
    project(NEXT)
    z_third(0)
    y_first(0, FAR)
    y_second(0, FAR)
    y_third(0, FAR)
    project(FAR)
    locals_[3].wait()
    locals_[4].wait()
    attend(0)
    z_first(1)
    attend(1)
    partials(OWN)
    sum_first(OWN)
    z_second(1)
    y_first(1, PREV)
    y_first(1, NEXT)
    y_second(1, PREV)
    y_second(1, NEXT)
    sum_second(OWN)
    y_third(1, PREV)
    y_third(1, NEXT)
    partials(PREV)
    sum_first(PREV)
    sum_third(OWN)
    partials(NEXT)
    sum_first(NEXT)
    z_third(1)
    y_first(1, FAR)
    sum_second(PREV)
    sum_second(NEXT)
    y_second(1, FAR)
    y_third(1, FAR)
    sum_third(PREV)
    sum_third(NEXT)
    partials(FAR)
    sum_first(FAR)
    gathered(OWN)
    sum_second(FAR)
    sum_third(FAR)
    gathered(PREV)
    gathered(NEXT)
    gathered(FAR)

    total = tot[...] + res_ref[...].astype(F32)
    hid_ref[...] = total.astype(BF16)
    mean_square = jnp.mean(total * total, axis=-1, keepdims=True)
    normed = total * lax.rsqrt(mean_square + norm_eps) * gain_ref[...].astype(F32)
    nbuf[ti] = normed.astype(BF16)

    def n_at(kx, o):
        return nbuf.at[ring(x, kx) * NZ + (zl - o) % NZ]

    def gx_start(o):
        s, r = gxs.at[o], gxr.at[o]
        push(n_at(OWN, o), s, r, 0, x_up)
        push(n_at(OWN, o), s, r, 1, x_dn)

    def gx_next(o):
        s, r = gxs.at[o], gxr.at[o]
        landed(n_at(PREV, o), s.at[0], r.at[0])
        push(n_at(PREV, o).at[:, :4096], s, r, 2, x_up)
        landed(n_at(NEXT, o), s.at[1], r.at[1])
        push(n_at(NEXT, o).at[:, 4096:], s, r, 3, x_dn)

    def gx_last(o):
        s, r = gxs.at[o], gxr.at[o]
        landed(n_at(FAR, o).at[:, :4096], s.at[2], r.at[2])
        landed(n_at(FAR, o).at[:, 4096:], s.at[3], r.at[3])

    order = (1, 7, 2, 6, 3, 5, 4)
    for o in order:
        push(nbuf.at[ti], gzs, gzr, o - 1, ten(x * NZ + (zl + o) % NZ))
    gx_start(0)
    before = 0
    for o in order:
        landed(n_at(OWN, o), gzs.at[o - 1], gzr.at[o - 1])
        gx_start(o)
        gx_next(before)
        before = o
    gx_next(before)
    outs = []

    def put(kx):
        rows = pl.ds(ring(x, kx) * NZ, NZ)
        copy = pltpu.make_async_copy(nbuf.at[rows], norm_hbm.at[rows], out_sem.at[kx])
        copy.start()
        outs.append(copy)

    put(OWN)
    put(PREV)
    put(NEXT)
    for o in (0, *order):
        gx_last(o)
    put(FAR)
    for copy in sent:
        copy.wait_send()
    for copy in outs:
        copy.wait()


def rope_tables(tok_count, ctx_len, head_dim):
    half = head_dim // 2
    inv_freq = np.float64(rope_theta) ** (-2.0 * np.arange(half) / head_dim)
    angles = (ctx_len - tok_count + np.arange(tok_count))[:, None] * inv_freq[None, :]
    cosine, sine = np.cos(angles), np.sin(angles)
    return (
        jnp.asarray(np.concatenate([cosine, cosine], axis=1), F32),
        jnp.asarray(np.concatenate([-sine, sine], axis=1), F32),
    )


def body(
    attn_input, residual, query_weight, query_bias, output_weight, cached_keys, cached_values,
    norm_gain,
):
    tok, width = attn_input.shape
    ctx_len, head_dim = cached_keys.shape[2:]
    own_count = tok // lax.axis_size("tensor")
    resid_rows = lax.dynamic_slice_in_dim(
        residual, lax.axis_index("tensor") * own_count, own_count, 0
    )
    cosine, sine = rope_tables(tok, ctx_len, head_dim)
    dma, vmem = pltpu.SemaphoreType.DMA, pltpu.VMEM
    any_spec = pl.BlockSpec(memory_space=pl.ANY)
    vmem_spec = pl.BlockSpec(memory_space=pltpu.VMEM)
    hidden, normed = pl.pallas_call(
        block_kernel,
        name="block",
        out_shape=(
            jax.ShapeDtypeStruct((own_count, width), BF16),
            jax.ShapeDtypeStruct((32, own_count, width), BF16),
        ),
        in_specs=[any_spec] * 5 + [vmem_spec] * 5,
        out_specs=(vmem_spec, any_spec),
        scratch_shapes=[
            vmem((2, 32, 2, 128, 256), BF16),
            vmem((tok, width), BF16),
            vmem((ctx_len, head_dim), BF16),
            vmem((ctx_len, head_dim), BF16),
            vmem((tok, 256), F32),
            vmem((tok, 256), BF16),
            vmem((4, 32, own_count, 2048), BF16),
            vmem((4, 2, 4, own_count, 2048), BF16),
            vmem((4, 2, 2, 4, own_count, 2048), BF16),
            vmem((4, 8, own_count, 2048), BF16),
            vmem((4, 7, own_count, 2048), BF16),
            vmem((own_count, width), F32),
            vmem((32, own_count, width), BF16),
            dma((5,)), dma((4,)),
            dma((2, 6)), dma((2, 6)),
            dma((2, 4, 6)), dma((2, 4, 6)),
            dma((2, 4, 4)), dma((2, 4, 4)),
            dma((4, 2)), dma((4, 2)),
            dma((4, 4)), dma((4, 4)),
            dma((4, 7)), dma((4, 7)),
            dma((7,)), dma((7,)),
            dma((8, 4)), dma((8, 4)),
        ],
        compiler_params=pltpu.CompilerParams(
            collective_id=0, has_side_effects=True, vmem_limit_bytes=48 * 1024 * 1024
        ),
    )(
        attn_input,
        query_weight.reshape(2, 128, 256),
        output_weight.reshape(2, 128, 256),
        cached_keys[0, 0],
        cached_values[0, 0],
        query_bias.reshape(1, -1),
        cosine,
        sine,
        resid_rows,
        norm_gain.reshape(1, -1),
    )
    return hidden, normed.reshape(tok, width)


def solution(mesh):
    return jax.shard_map(
        body,
        mesh=mesh,
        in_specs=(
            P("dp", None),
            P("dp", None),
            P("dp", "tensor"),
            P("tensor"),
            P("tensor", "dp"),
            P("dp", "tensor", None, None),
            P("dp", "tensor", None, None),
            P(),
        ),
        out_specs=(P(("dp", "tensor"), None), P("dp", None)),
        check_vma=False,
    )
```

time: 535 us -> 188 us (0.35)
  the two profiles are of different devices: /device:TPU:40 before, /device:TPU:96 now
where the time goes in v1:
time: 188 us
  Pallas kernels  173 us (92%)
  local copies, waits for them, and re-layouts  14.5 us (8%)
    pallas_call x1, Pallas kernels, body(): pl.pallas_call(block_kernel, name='block', out_shape=(jax.ShapeDtypeStruc...  173 us
    unnamed x19, local copies, waits for them, and re-layouts  8.99 us
    reshape x1, local copies, waits for them, and re-layouts, body(): return (hidden, normed.reshape(tok, width))  3.94 us

profile of v1, /device:TPU:96, one launch (start us, length us, event | category | flops | bytes accessed | tf_op | source)
XLA Modules:
  0.0 187.9 jit_solution(10176020442302518889)
XLA Ops:
  0.6 0.0 copy-start
  0.6 0.8 reshape.21.bias_ref
  1.5 0.7 reshape.22.gain_ref
  2.2 0.0 copy-done
  2.3 0.0 copy-start.1
  2.3 1.6 copy-done.1
  3.9 0.0 copy-start.3
  3.9 0.9 copy-done.3
  4.8 0.0 copy-start.4
  4.8 0.9 copy-done.4
  5.8 0.0 copy-start.5
  5.8 0.9 copy-done.5
  6.7 0.0 copy-start.6
  6.7 0.9 copy-done.6
  7.6 0.0 copy-start.7
  7.6 0.8 copy-done.7
  8.4 0.0 copy-start.8
  8.4 0.8 copy-done.8
  9.3 172.7 %block.1 = (bf16[4,8192]{1,0:T(4,128)(2,1)S(1)}, bf16[32,4,8192]{2,1,0:T(4,128)(2,1)S(1)}) custom-call(bf16[128,8192]{1,0:T(8,128)(2,1)S(1)} %copy-done.1, bf16[2,128,256]{2,1,0:T(8,128)(2,1)S(1)} %bitcast.6, bf16[2,128,256]{2,1,0:T(8,128)(2,1)S(1)} %bitcast.7, bf16[1024,128]{1,0:T(8,128)(2,1)S(1)} %bitcast.4, bf16[1024,128]{1,0:T(8,128)(2,1)S(1)} %bitcast.5, ...), custom_call_target="tpu_custom_call" | custom-call | tf_op jit(solution)/shard_map/block/pallas_call | solution.py:391
  181.9 0.0 copy-start.2
  182.0 1.3 copy-done.2
  183.3 3.9 %reshape.23 = bf16[128,8192]{1,0:T(8,128)(2,1)} reshape(bf16[32,4,8192]{2,1,0:T(4,128)(2,1)} %copy-done.2) | data formatting | bytes 4194304 | tf_op jit(solution)/shard_map/reshape | solution.py:439
  187.2 0.6 copy.13
  (1 shorter events, 0.0 us)
Async XLA Ops:
  0.6 1.6 copy-start
  2.3 1.6 copy-start.1
  3.9 0.9 copy-start.3
  4.8 0.9 copy-start.4
  5.8 0.9 copy-start.5
  6.7 0.9 copy-start.6
  7.6 0.8 copy-start.7
  8.4 0.8 copy-start.8
  181.9 1.3 copy-start.2

commit v2 on v0

v2 whole, which is shorter than its diff:
```python
import jax
import jax.numpy as jnp
import numpy as np
from jax import lax
from jax.experimental import pallas as pl
from jax.experimental.pallas import tpu as pltpu
from jax.sharding import PartitionSpec as P

rope_theta = 1000000.0
norm_eps = 1e-06

NY, NH, NC = 4, 4, 2
NX, NZ = 4, 8
OWN, PREV, NEXT, FAR = 0, 1, 2, 3
STEP = (0, 3, 1, 2)
GROUP = ((0, 0), (1, 0), (1, 2048), (2, 0))
F32, BF16 = jnp.float32, jnp.bfloat16


def block_kernel(
    x_hbm, wq_hbm, wo_hbm, k_hbm, v_hbm, rope_hbm, res_hbm, bias_ref, gain_ref,
    hid_hbm, norm_hbm,
    wq, wo, xv, kv, vv, rope, resv, q, mixed, part, x1, x2, xsum, zr1, zmid, zr2, zacc, tot,
    n0, n1, n2, stage, hid, gain,
    loc, out_sem, zqs, zqr, yqs, yqr, dqs, dqr, zos, zor, yos, yor, dos, dor,
    p1s, p1r, p2s, p2r, t1s, t1r, t2s, t2r, gzs, gzr, gxs, gxr,
):
    dp = lax.axis_index("dp")
    ti = lax.axis_index("tensor")
    y, h, c = dp // (NH * NC), (dp // NC) % NH, dp % NC
    x, zl = ti // NZ, ti % NZ
    zq, zi = zl // 4, zl % 4

    def piece(yy, hh, cc):
        return yy * (NH * NC) + hh * NC + cc

    def ring(base, slot):
        return (base + STEP[slot]) % 4

    def dev(d):
        return {"dp": d}

    def ten(xx, quad, place):
        return {"tensor": xx * NZ + quad * 4 + place}

    h_up, h_dn = dev(piece(y, ring(h, NEXT), c)), dev(piece(y, ring(h, PREV), c))
    y_up, y_dn = dev(piece(ring(y, NEXT), h, c)), dev(piece(ring(y, PREV), h, c))
    sib = dev(piece(y, h, 1 - c))
    x_up, x_dn = ten(ring(x, NEXT), zq, zi), ten(ring(x, PREV), zq, zi)
    nb = (n0, n1, n2)
    mates = [None] + [ten(x, zq, (zi + o) % 4) for o in range(1, 4)]
    across = ten(x, 1 - zq, zi)

    locals_ = [
        pltpu.make_async_copy(wq_hbm, wq.at[dp], loc.at[0]),
        pltpu.make_async_copy(wo_hbm.at[:, :, :128], wo.at[dp, 0], loc.at[1]),
        pltpu.make_async_copy(wo_hbm.at[:, :, 128:], wo.at[dp, 1], loc.at[2]),
        pltpu.make_async_copy(x_hbm, xv, loc.at[3]),
        pltpu.make_async_copy(k_hbm, kv, loc.at[4]),
        pltpu.make_async_copy(v_hbm, vv, loc.at[5]),
        pltpu.make_async_copy(rope_hbm, rope, loc.at[6]),
        pltpu.make_async_copy(
            res_hbm.at[pl.ds(pl.multiple_of(ti // 2 * 8, 8), 8)], resv, loc.at[7]
        ),
    ]
    for copy in locals_:
        copy.start()

    barrier = pltpu.get_barrier_semaphore()
    partners = [h_up, h_dn, y_up, y_dn, sib, x_up, x_dn, across, *mates[1:]]
    for partner in partners:
        pl.semaphore_signal(
            barrier, inc=1, device_id=partner, device_id_type=pl.DeviceIdType.MESH
        )
    q[...] = jnp.zeros_like(q)
    for copy in locals_[:3]:
        copy.wait()
    pl.semaphore_wait(barrier, len(partners))

    sent = []

    def remote(src, dst, send_sem, recv_sem, target):
        return pltpu.make_async_remote_copy(
            src_ref=src, dst_ref=dst, send_sem=send_sem, recv_sem=recv_sem,
            device_id=target, device_id_type=pl.DeviceIdType.MESH,
        )

    def send(src, dst, send_sem, recv_sem, target):
        copy = remote(src, dst, send_sem, recv_sem, target)
        copy.start()
        sent.append(copy)
        return copy

    def left(*copies):
        for copy in copies:
            copy.wait_send()
            sent[:] = [other for other in sent if other is not copy]

    def landed(dst, send_sem, recv_sem):
        remote(dst, dst, send_sem, recv_sem, sib).wait_recv()

    def push(ref, s, r, i, target):
        return send(ref, ref, s.at[i], r.at[i], target)

    def q_at(ky, kh, half):
        return wq.at[piece(ring(y, ky), ring(h, kh), c), half]

    def q_start():
        return push(q_at(OWN, OWN, 0), zqs, zqr, 0, h_up), push(
            q_at(OWN, OWN, 1), zqs, zqr, 3, h_dn
        )

    def q_start_rest():
        push(q_at(OWN, OWN, 1), zqs, zqr, 1, h_up)
        push(q_at(OWN, OWN, 0), zqs, zqr, 4, h_dn)

    def qy_start(k, half):
        s, r = yqs.at[k], yqr.at[k]
        if half == 0:
            push(q_at(OWN, k, 0), s, r, 0, y_up)
            push(q_at(OWN, k, 0), s, r, 4, y_dn)
        else:
            push(q_at(OWN, k, 1), s, r, 3, y_dn)
            push(q_at(OWN, k, 1), s, r, 1, y_up)

    def qd_start(k, ky):
        push(wq.at[piece(ring(y, ky), ring(h, k), c)], dqs.at[k], dqr.at[k], ky, sib)

    def q_first():
        landed(q_at(OWN, PREV, 0), zqs.at[0], zqr.at[0])
        push(q_at(OWN, PREV, 0), zqs, zqr, 2, h_up)
        landed(q_at(OWN, NEXT, 1), zqs.at[3], zqr.at[3])
        push(q_at(OWN, NEXT, 1), zqs, zqr, 5, h_dn)
        qy_start(PREV, 0)
        qy_start(NEXT, 1)

    def q_second():
        landed(q_at(OWN, PREV, 1), zqs.at[1], zqr.at[1])
        qy_start(PREV, 1)
        qd_start(PREV, OWN)
        landed(q_at(OWN, NEXT, 0), zqs.at[4], zqr.at[4])
        qy_start(NEXT, 0)
        qd_start(NEXT, OWN)

    def q_third():
        landed(q_at(OWN, FAR, 0), zqs.at[2], zqr.at[2])
        qy_start(FAR, 0)
        landed(q_at(OWN, FAR, 1), zqs.at[5], zqr.at[5])
        qy_start(FAR, 1)
        qd_start(FAR, OWN)

    def qy_up(k):
        landed(q_at(PREV, k, 0), yqs.at[k, 0], yqr.at[k, 0])
        push(q_at(PREV, k, 0), yqs.at[k], yqr.at[k], 2, y_up)

    def qy_dn(k):
        landed(q_at(NEXT, k, 1), yqs.at[k, 3], yqr.at[k, 3])
        push(q_at(NEXT, k, 1), yqs.at[k], yqr.at[k], 5, y_dn)

    def qy_second(k):
        s, r = yqs.at[k], yqr.at[k]
        landed(q_at(PREV, k, 1), s.at[1], r.at[1])
        qd_start(k, PREV)
        landed(q_at(NEXT, k, 0), s.at[4], r.at[4])
        qd_start(k, NEXT)

    def qy_third(k):
        s, r = yqs.at[k], yqr.at[k]
        landed(q_at(FAR, k, 0), s.at[2], r.at[2])
        landed(q_at(FAR, k, 1), s.at[5], r.at[5])
        qd_start(k, FAR)

    def o_at(ky, kh, a):
        return wo.at[piece(ring(y, ky), ring(h, kh), c), a]

    def o_start(a):
        push(o_at(OWN, OWN, a), zos, zor, 2 * a, h_up)
        push(o_at(OWN, OWN, a), zos, zor, 2 * a + 1, h_dn)

    def oy_start(k, a):
        push(o_at(OWN, k, a), yos.at[k, a], yor.at[k, a], 0, y_up)
        push(o_at(OWN, k, a), yos.at[k, a], yor.at[k, a], 1, y_dn)

    def od_start(k, a, ky):
        push(o_at(ky, k, a), dos.at[k, a], dor.at[k, a], ky, sib)

    def o_first(a):
        landed(o_at(OWN, PREV, a), zos.at[2 * a], zor.at[2 * a])
        push(o_at(OWN, PREV, a).at[0], zos, zor, 4 + 2 * a, h_up)
        landed(o_at(OWN, NEXT, a), zos.at[2 * a + 1], zor.at[2 * a + 1])
        push(o_at(OWN, NEXT, a).at[1], zos, zor, 5 + 2 * a, h_dn)
        for k in (PREV, NEXT):
            oy_start(k, a)
            od_start(k, a, OWN)

    def o_third(a):
        landed(o_at(OWN, FAR, a).at[0], zos.at[4 + 2 * a], zor.at[4 + 2 * a])
        landed(o_at(OWN, FAR, a).at[1], zos.at[5 + 2 * a], zor.at[5 + 2 * a])
        oy_start(FAR, a)
        od_start(FAR, a, OWN)

    def oy_first(k, a):
        s, r = yos.at[k, a], yor.at[k, a]
        landed(o_at(PREV, k, a), s.at[0], r.at[0])
        push(o_at(PREV, k, a).at[0], s, r, 2, y_up)
        od_start(k, a, PREV)
        landed(o_at(NEXT, k, a), s.at[1], r.at[1])
        push(o_at(NEXT, k, a).at[1], s, r, 3, y_dn)
        od_start(k, a, NEXT)

    def oy_third(k, a):
        s, r = yos.at[k, a], yor.at[k, a]
        landed(o_at(FAR, k, a).at[0], s.at[2], r.at[2])
        landed(o_at(FAR, k, a).at[1], s.at[3], r.at[3])
        od_start(k, a, FAR)

    def project(k):
        hk = ring(h, k)
        for ky in range(4):
            ref = wq.at[piece(ring(y, ky), hk, 1 - c)]
            landed(ref, dqs.at[k, ky], dqr.at[k, ky])

        acc = q[...]
        for j in range(NY * NC):
            d = piece(j // NC, hk, j % NC)
            cols = xv[:, pl.ds(pl.multiple_of(d * 256, 256), 256)]
            acc = acc + jnp.dot(cols, wq[d].reshape(256, 256), preferred_element_type=F32)
        q[...] = acc

    def attend(head):
        cols = slice(head * 128, head * 128 + 128)
        proj = q[:, cols] + bias_ref[cols].astype(F32).reshape(1, 128)
        turned = proj * rope[0] + pltpu.roll(proj, 64, 1) * rope[1]
        scores = lax.dot_general(
            turned.astype(BF16), kv[...], (((1,), (1,)), ((), ())), preferred_element_type=F32
        ) * (1.0 / 128**0.5)
        rows = lax.broadcasted_iota(jnp.int32, scores.shape, 0)
        keys = lax.broadcasted_iota(jnp.int32, scores.shape, 1)
        scores = jnp.where(keys <= rows + (scores.shape[1] - scores.shape[0]), scores, -1e30)
        expo = jnp.exp(scores - jnp.max(scores, axis=-1, keepdims=True))
        soft = (expo / jnp.sum(expo, axis=-1, keepdims=True)).astype(BF16)
        mixed[:, cols] = jnp.dot(soft, vv[...], preferred_element_type=F32).astype(BF16)

    def partials(k, a):
        hk = ring(h, k)
        for ky in range(4):
            ref = wo.at[piece(ring(y, ky), hk, 1 - c), a]
            landed(ref, dos.at[k, a, ky], dor.at[k, a, ky])

        for j in range(NY * NC):
            d = piece(j // NC, hk, j % NC)
            out = jnp.dot(mixed[...], wo[d, a].reshape(256, 128), preferred_element_type=F32)
            part[k, a, :, :, j * 128 : j * 128 + 128] = out.astype(BF16).reshape(32, 4, 128)

    def rows_of(k, a, slot, at):
        return part.at[k, a, pl.ds(ring(x, slot) * NZ + at, 4)]

    def sum_first(k, a):
        s, r = p1s.at[k, a], p1r.at[k, a]
        send(rows_of(k, a, FAR, 0), x1.at[k, a, 0], s.at[0], r.at[0], x_up)
        send(rows_of(k, a, FAR, 4), x1.at[k, a, 1], s.at[1], r.at[1], x_dn)
        s, r = p2s.at[k, a], p2r.at[k, a]
        send(rows_of(k, a, NEXT, 4), x2.at[k, a, 0, 1], s.at[0], r.at[0], x_up)
        send(rows_of(k, a, PREV, 0), x2.at[k, a, 1, 0], s.at[1], r.at[1], x_dn)

    def sum_second(k, a):
        s, r = p2s.at[k, a], p2r.at[k, a]
        landed(x1.at[k, a, 0], p1s.at[k, a, 0], p1r.at[k, a, 0])
        own = rows_of(k, a, NEXT, 0)
        own[...] = (own[...].astype(F32) + x1[k, a, 0].astype(F32)).astype(BF16)
        send(own, x2.at[k, a, 0, 0], s.at[2], r.at[2], x_up)
        landed(x1.at[k, a, 1], p1s.at[k, a, 1], p1r.at[k, a, 1])
        own = rows_of(k, a, PREV, 4)
        own[...] = (own[...].astype(F32) + x1[k, a, 1].astype(F32)).astype(BF16)
        send(own, x2.at[k, a, 1, 1], s.at[3], r.at[3], x_dn)

    def sum_third(k, a):
        s, r = p2s.at[k, a], p2r.at[k, a]
        landed(x2.at[k, a, 0, 1], s.at[0], r.at[0])
        landed(x2.at[k, a, 1, 0], s.at[1], r.at[1])
        landed(x2.at[k, a, 0, 0], s.at[2], r.at[2])
        landed(x2.at[k, a, 1, 1], s.at[3], r.at[3])
        for half in range(2):
            own = rows_of(k, a, OWN, half * 4)[...].astype(F32)
            both = x2[k, a, 0, half].astype(F32) + x2[k, a, 1, half].astype(F32)
            xsum[k, a, half] = (own + both).astype(BF16)
        s, r = t1s.at[k, a], t1r.at[k, a]
        for o in range(1, 4):
            send(xsum.at[k, a, :, (zi + o) % 4], zr1.at[k, a, o - 1], s.at[o - 1], r.at[o - 1],
                 mates[o])

    def sum_fourth(k, a):
        for o in range(3):
            landed(zr1.at[k, a, o], t1s.at[k, a, o], t1r.at[k, a, o])

        def quad_sum(quad):
            acc = xsum[k, a, quad, zi].astype(F32)
            for o in range(3):
                acc = acc + zr1[k, a, o, quad].astype(F32)
            return acc

        zmid[k, a] = quad_sum(1 - zq).astype(BF16)
        send(zmid.at[k, a], zr2.at[k, a], t2s.at[k, a], t2r.at[k, a], across)
        zacc[k, a] = quad_sum(zq)

    def gathered(k, a):
        landed(zr2.at[k, a], t2s.at[k, a], t2r.at[k, a])
        acc = zacc[k, a] + zr2[k, a].astype(F32)
        hk = ring(h, k)
        g, base = GROUP[k]
        for j in range(NY * NC):
            d = piece(j // NC, hk, j % NC)
            at = pl.ds(pl.multiple_of(d * 256 + a * 128, 128), 128)
            total = tot[:, at] + acc[:, j * 128 : j * 128 + 128]
            tot[:, at] = total
            to = base + a * 1024 + j * 128
            nb[g][ti, :, to : to + 128] = total.astype(BF16)

    def n_at(g, kx, other, o):
        quad = (zq + other) % 2
        return nb[g].at[ring(x, kx) * NZ + quad * 4 + (zi + 4 - o) % 4]

    def gx_start(g, other, o):
        s, r = gxs.at[g, other, o], gxr.at[g, other, o]
        push(n_at(g, OWN, other, o), s, r, 0, x_up)
        push(n_at(g, OWN, other, o), s, r, 1, x_dn)

    def gx_next(g, other, o):
        s, r = gxs.at[g, other, o], gxr.at[g, other, o]
        half = nb[g].shape[-1] // 2
        landed(n_at(g, PREV, other, o), s.at[0], r.at[0])
        push(n_at(g, PREV, other, o).at[:, :half], s, r, 2, x_up)
        landed(n_at(g, NEXT, other, o), s.at[1], r.at[1])
        push(n_at(g, NEXT, other, o).at[:, half:], s, r, 3, x_dn)

    def gx_last(g, other, o):
        s, r = gxs.at[g, other, o], gxr.at[g, other, o]
        half = nb[g].shape[-1] // 2
        landed(n_at(g, FAR, other, o).at[:, :half], s.at[2], r.at[2])
        landed(n_at(g, FAR, other, o).at[:, half:], s.at[3], r.at[3])

    def gz_landed(g, other, o):
        landed(n_at(g, OWN, other, o), gzs.at[g, other, o], gzr.at[g, other, o])
        gx_start(g, other, o)

    def g_start(g):
        mine = n_at(g, OWN, 0, 0)
        send(mine, mine, gzs.at[g, 1, 0], gzr.at[g, 1, 0], across)
        for o in (1, 3, 2):
            push(mine, gzs.at[g, 0], gzr.at[g, 0], o, mates[o])
        gx_start(g, 0, 0)

    def g_across(g):
        gz_landed(g, 1, 0)
        for o in (1, 3, 2):
            push(n_at(g, OWN, 1, 0), gzs.at[g, 1], gzr.at[g, 1], o, mates[o])

    def g_quad(g, other):
        for o in (1, 3, 2):
            gz_landed(g, other, o)

    def g_ring(g, other):
        for o in (0, 1, 3, 2):
            gx_next(g, other, o)

    def put(kx):
        slot = ring(x, kx)
        rows8 = pl.ds(slot * NZ, NZ)
        hi, lo = nb[2][rows8, :, 2048:2176], nb[2][rows8, :, 2176:2304]
        scale = (hi.astype(F32) + lo.astype(F32)).reshape(32, 128)
        rows32 = pl.ds(pl.multiple_of(slot * 32, 32), 32)
        for k in range(4):
            hk = ring(h, k)
            g, base = GROUP[k]

            def one(i, carry, g=g, base=base, hk=hk):
                a, j = i // 8, i % 8
                d = piece(j // NC, hk, j % NC)
                at = pl.ds(pl.multiple_of(d * 256 + a * 128, 128), 128)
                src = pl.ds(pl.multiple_of(base + i * 128, 128), 128)
                vals = nb[g][rows8, :, src].astype(F32).reshape(32, 128)
                stage[rows32, at] = (vals * scale * gain[:, at]).astype(BF16)
                return carry

            lax.fori_loop(0, 16, one, 0, unroll=4)
        copy = pltpu.make_async_copy(stage.at[rows32], norm_hbm.at[rows32], out_sem.at[kx])
        copy.start()
        outs.append(copy)

    first = q_start()
    qy_start(OWN, 0)
    qy_start(OWN, 1)
    qd_start(OWN, OWN)
    qy_up(OWN)
    qy_dn(OWN)
    for a in range(2):
        oy_start(OWN, a)
        od_start(OWN, a, OWN)
    qy_second(OWN)
    qy_third(OWN)
    left(*first)
    q_start_rest()
    oy_first(OWN, 0)
    oy_first(OWN, 1)
    locals_[3].wait()
    project(OWN)
    locals_[7].wait()
    resid = resv[...].astype(F32)
    tot[...] = jnp.where(ti % 2 == 0, resid[:4], resid[4:])
    gain[...] = gain_ref[...].astype(F32).reshape(1, -1)
    oy_third(OWN, 0)
    oy_third(OWN, 1)
    q_first()
    qy_up(PREV)
    qy_dn(NEXT)
    q_second()
    o_start(0)
    qy_dn(PREV)
    qy_up(NEXT)
    for k in (PREV, NEXT):
        qy_second(k)
    for k in (PREV, NEXT):
        qy_third(k)
    project(PREV)
    project(NEXT)
    q_third()
    o_start(1)
    qy_up(FAR)
    qy_dn(FAR)
    qy_second(FAR)
    qy_third(FAR)
    project(FAR)
    locals_[4].wait()
    locals_[5].wait()
    locals_[6].wait()
    attend(0)
    attend(1)
    for a in range(2):
        partials(OWN, a)
        sum_first(OWN, a)
    o_first(0)
    for a in range(2):
        sum_second(OWN, a)
    for k in (PREV, NEXT):
        oy_first(k, 0)
    o_first(1)
    for a in range(2):
        sum_third(OWN, a)
    for k in (PREV, NEXT):
        oy_third(k, 0)
    for k in (PREV, NEXT):
        partials(k, 0)
        sum_first(k, 0)
    o_third(0)
    for k in (PREV, NEXT):
        oy_first(k, 1)
    for k in (PREV, NEXT):
        sum_second(k, 0)
    oy_first(FAR, 0)
    for k in (PREV, NEXT):
        oy_third(k, 1)
        partials(k, 1)
        sum_first(k, 1)
    for k in (PREV, NEXT):
        sum_third(k, 0)
    oy_third(FAR, 0)
    partials(FAR, 0)
    sum_first(FAR, 0)
    o_third(1)
    for k in (PREV, NEXT):
        sum_second(k, 1)
    for a in range(2):
        sum_fourth(OWN, a)
    for k in (PREV, NEXT):
        sum_third(k, 1)
    oy_first(FAR, 1)
    sum_second(FAR, 0)
    oy_third(FAR, 1)
    partials(FAR, 1)
    sum_first(FAR, 1)
    sum_third(FAR, 0)
    for a in range(2):
        gathered(OWN, a)
    g_start(0)
    for k in (PREV, NEXT):
        sum_fourth(k, 0)
    sum_second(FAR, 1)
    for k in (PREV, NEXT):
        sum_fourth(k, 1)
    sum_third(FAR, 1)
    sum_fourth(FAR, 0)
    g_quad(0, 0)
    g_across(0)
    for k in (PREV, NEXT):
        for a in range(2):
            gathered(k, a)
    g_start(1)
    sum_fourth(FAR, 1)
    gathered(FAR, 0)
    gathered(FAR, 1)
    total = tot[...]
    mean_square = jnp.mean(total * total, axis=-1, keepdims=True)
    scale = jnp.broadcast_to(lax.rsqrt(mean_square + norm_eps), (4, 128))
    high = scale.astype(BF16)
    nb[2][ti, :, 2048:2176] = high
    nb[2][ti, :, 2176:2304] = (scale - high.astype(F32)).astype(BF16)
    g_start(2)
    hid[...] = total.astype(BF16)
    outs = [pltpu.make_async_copy(hid, hid_hbm, out_sem.at[4])]
    outs[0].start()
    g_quad(1, 0)
    g_across(1)
    g_ring(0, 0)
    g_quad(0, 1)
    g_quad(2, 0)
    g_across(2)
    g_ring(1, 0)
    g_ring(0, 1)
    g_quad(1, 1)
    g_ring(2, 0)
    g_quad(2, 1)
    g_ring(1, 1)
    g_ring(2, 1)
    put(OWN)
    put(PREV)
    put(NEXT)
    for g in range(3):
        for other in range(2):
            for o in (0, 1, 3, 2):
                gx_last(g, other, o)
    put(FAR)
    for copy in sent:
        copy.wait_send()
    for copy in outs:
        copy.wait()


def rope_tables(tok_count, ctx_len, head_dim):
    half = head_dim // 2
    inv_freq = np.float64(rope_theta) ** (-2.0 * np.arange(half) / head_dim)
    angles = (ctx_len - tok_count + np.arange(tok_count))[:, None] * inv_freq[None, :]
    cosine, sine = np.cos(angles), np.sin(angles)
    cosine, sine = np.concatenate([cosine, cosine], 1), np.concatenate([-sine, sine], 1)
    return jnp.asarray(np.stack([cosine, sine]), F32)


def body(
    attn_input, residual, query_weight, query_bias, output_weight, cached_keys, cached_values,
    norm_gain,
):
    tok, width = attn_input.shape
    ctx_len, head_dim = cached_keys.shape[2:]
    own_count = tok // lax.axis_size("tensor")
    dma, vmem = pltpu.SemaphoreType.DMA, pltpu.VMEM
    any_spec = pl.BlockSpec(memory_space=pl.ANY)
    vmem_spec = pl.BlockSpec(memory_space=pltpu.VMEM)
    twice = lambda *shape: [dma(shape), dma(shape)]
    return pl.pallas_call(
        block_kernel,
        name="block",
        out_shape=(
            jax.ShapeDtypeStruct((own_count, width), BF16),
            jax.ShapeDtypeStruct((tok, width), BF16),
        ),
        in_specs=[any_spec] * 7 + [vmem_spec] * 2,
        out_specs=(any_spec, any_spec),
        scratch_shapes=[
            vmem((32, 2, 128, 256), BF16),
            vmem((32, 2, 2, 128, 128), BF16),
            vmem((tok, width), BF16),
            vmem((ctx_len, head_dim), BF16),
            vmem((ctx_len, head_dim), BF16),
            vmem((2, tok, head_dim), F32),
            vmem((8, width), BF16),
            vmem((tok, 256), F32),
            vmem((tok, 256), BF16),
            vmem((4, 2, 32, own_count, 1024), BF16),
            vmem((4, 2, 2, 4, own_count, 1024), BF16),
            vmem((4, 2, 2, 2, 4, own_count, 1024), BF16),
            vmem((4, 2, 2, 4, own_count, 1024), BF16),
            vmem((4, 2, 3, 2, own_count, 1024), BF16),
            vmem((4, 2, own_count, 1024), BF16),
            vmem((4, 2, own_count, 1024), BF16),
            vmem((4, 2, own_count, 1024), F32),
            vmem((own_count, width), F32),
            vmem((32, own_count, 2048), BF16),
            vmem((32, own_count, 4096), BF16),
            vmem((32, own_count, 2304), BF16),
            vmem((tok, width), BF16),
            vmem((own_count, width), BF16),
            vmem((1, width), F32),
            dma((8,)), dma((5,)),
            *twice(6), *twice(4, 6), *twice(4, 4),
            *twice(8), *twice(4, 2, 4), *twice(4, 2, 4),
            *twice(4, 2, 2), *twice(4, 2, 4), *twice(4, 2, 3), *twice(4, 2),
            *twice(3, 2, 4), *twice(3, 2, 4, 4),
        ],
        compiler_params=pltpu.CompilerParams(
            collective_id=0, has_side_effects=True, vmem_limit_bytes=67043328
        ),
    )(
        attn_input,
        query_weight.reshape(2, 128, 256),
        output_weight.reshape(2, 128, 256),
        cached_keys[0, 0],
        cached_values[0, 0],
        rope_tables(tok, ctx_len, head_dim),
        residual,
        query_bias,
        norm_gain,
    )


def solution(mesh):
    return jax.shard_map(
        body,
        mesh=mesh,
        in_specs=(
            P("dp", None),
            P("dp", None),
            P("dp", "tensor"),
            P("tensor"),
            P("tensor", "dp"),
            P("dp", "tensor", None, None),
            P("dp", "tensor", None, None),
            P(),
        ),
        out_specs=(P(("dp", "tensor"), None), P("dp", None)),
        check_vma=False,
    )
```

time: 535 us -> 170 us (0.32)
  the two profiles are of different devices: /device:TPU:40 before, /device:TPU:32 now
where the time goes in v2:
time: 170 us
  Pallas kernels  165 us (97%)
  local copies, waits for them, and re-layouts  4.59 us (3%)
    pallas_call x1, Pallas kernels, body(): pl.pallas_call(block_kernel, name='block', out_shape=(jax.ShapeDtypeStruc...  165 us
    unnamed x2, local copies, waits for them, and re-layouts  4.59 us

profile of v2, /device:TPU:32, one launch (start us, length us, event | category | flops | bytes accessed | tf_op | source)
XLA Modules:
  0.0 169.8 jit_solution(15290210962792002171)
XLA Ops:
  0.6 164.6 %block.1 = (bf16[4,8192]{1,0:T(4,128)(2,1)}, bf16[128,8192]{1,0:T(8,128)(2,1)}) custom-call(bf16[128,8192]{1,0:T(8,128)(2,1)} %x_hbm.1, bf16[2,128,256]{2,1,0:T(8,128)(2,1)} %bitcast.6, bf16[2,128,256]{2,1,0:T(8,128)(2,1)} %bitcast.7, bf16[1024,128]{1,0:T(8,128)(2,1)} %bitcast.4, bf16[1024,128]{1,0:T(8,128)(2,1)} %bitcast.5, ...), custom_call_target="tpu_custom_call" | custom-call | tf_op jit(solution)/shard_map/block/pallas_call | solution.py:558
  165.2 1.5 copy.13
  166.7 3.1 %copy.14 = bf16[128,8192]{1,0:T(8,128)(2,1)} copy(bf16[128,8192]{1,0:T(8,128)(2,1)} %get-tuple-element.5) | data formatting | bytes 4194304

commit v3 on v2

--- a/solution.py
+++ b/solution.py
@@ -13,8 +13,17 @@
 NX, NZ = 4, 8
 OWN, PREV, NEXT, FAR = 0, 1, 2, 3
 STEP = (0, 3, 1, 2)
+INSIDE = tuple((other, o) for other in range(2) for o in range(4))
 GROUP = ((0, 0), (1, 0), (1, 2048), (2, 0))
 F32, BF16 = jnp.float32, jnp.bfloat16
+
+
+class Shared:
+    def __init__(self, index, own=None):
+        self.index, self.own, self.at = index, own or {}, self
+
+    def __getitem__(self, i):
+        return Shared(self.own[i]) if i in self.own else self
 
 
 def block_kernel(
@@ -22,8 +31,7 @@
     hid_hbm, norm_hbm,
     wq, wo, xv, kv, vv, rope, resv, q, mixed, part, x1, x2, xsum, zr1, zmid, zr2, zacc, tot,
     n0, n1, n2, stage, hid, gain,
-    loc, out_sem, zqs, zqr, yqs, yqr, dqs, dqr, zos, zor, yos, yor, dos, dor,
-    p1s, p1r, p2s, p2r, t1s, t1r, t2s, t2r, gzs, gzr, gxs, gxr,
+    loc, out_sem, left_sem, zqr, yqr, dqr, zor, yor, dor, p1r, p2r, t1r, t2r, gzr, gxr,
 ):
     dp = lax.axis_index("dp")
     ti = lax.axis_index("tensor")
@@ -77,7 +85,10 @@
         copy.wait()
     pl.semaphore_wait(barrier, len(partners))
 
-    sent = []
+    zqs, yqs, dqs = Shared(0, {0: 1, 3: 2, 2: 3, 5: 4}), Shared(0), Shared(0)
+    zos, yos, dos = Shared(5), Shared(5), Shared(5)
+    p1s, p2s, t1s, t2s = Shared(6), Shared(6), Shared(7), Shared(8)
+    gzs = gxs = Shared(9, {(g, *at): 9 + g for g in range(3) for at in INSIDE})
 
     def remote(src, dst, send_sem, recv_sem, target):
         return pltpu.make_async_remote_copy(
@@ -86,18 +97,16 @@
         )
 
     def send(src, dst, send_sem, recv_sem, target):
-        copy = remote(src, dst, send_sem, recv_sem, target)
+        copy = remote(src, dst, left_sem.at[send_sem.index], recv_sem, target)
         copy.start()
-        sent.append(copy)
         return copy
 
     def left(*copies):
         for copy in copies:
             copy.wait_send()
-            sent[:] = [other for other in sent if other is not copy]
 
     def landed(dst, send_sem, recv_sem):
-        remote(dst, dst, send_sem, recv_sem, sib).wait_recv()
+        remote(dst, dst, left_sem.at[send_sem.index], recv_sem, sib).wait_recv()
 
     def push(ref, s, r, i, target):
         return send(ref, ref, s.at[i], r.at[i], target)
@@ -128,11 +137,12 @@
 
     def q_first():
         landed(q_at(OWN, PREV, 0), zqs.at[0], zqr.at[0])
-        push(q_at(OWN, PREV, 0), zqs, zqr, 2, h_up)
+        up = push(q_at(OWN, PREV, 0), zqs, zqr, 2, h_up)
         landed(q_at(OWN, NEXT, 1), zqs.at[3], zqr.at[3])
-        push(q_at(OWN, NEXT, 1), zqs, zqr, 5, h_dn)
+        dn = push(q_at(OWN, NEXT, 1), zqs, zqr, 5, h_dn)
         qy_start(PREV, 0)
         qy_start(NEXT, 1)
+        return up, dn
 
     def q_second():
         landed(q_at(OWN, PREV, 1), zqs.at[1], zqr.at[1])
@@ -261,37 +271,33 @@
         send(rows_of(k, a, FAR, 4), x1.at[k, a, 1], s.at[1], r.at[1], x_dn)
         s, r = p2s.at[k, a], p2r.at[k, a]
         send(rows_of(k, a, NEXT, 4), x2.at[k, a, 0, 1], s.at[0], r.at[0], x_up)
-        send(rows_of(k, a, PREV, 0), x2.at[k, a, 1, 0], s.at[1], r.at[1], x_dn)
+        send(rows_of(k, a, PREV, 0), x2.at[k, a, 1, 0], s.at[1], r.at[0], x_dn)
 
     def sum_second(k, a):
         s, r = p2s.at[k, a], p2r.at[k, a]
         landed(x1.at[k, a, 0], p1s.at[k, a, 0], p1r.at[k, a, 0])
         own = rows_of(k, a, NEXT, 0)
         own[...] = (own[...].astype(F32) + x1[k, a, 0].astype(F32)).astype(BF16)
-        send(own, x2.at[k, a, 0, 0], s.at[2], r.at[2], x_up)
+        send(own, x2.at[k, a, 0, 0], s.at[2], r.at[0], x_up)
         landed(x1.at[k, a, 1], p1s.at[k, a, 1], p1r.at[k, a, 1])
         own = rows_of(k, a, PREV, 4)
         own[...] = (own[...].astype(F32) + x1[k, a, 1].astype(F32)).astype(BF16)
-        send(own, x2.at[k, a, 1, 1], s.at[3], r.at[3], x_dn)
+        send(own, x2.at[k, a, 1, 1], s.at[3], r.at[0], x_dn)
 
     def sum_third(k, a):
         s, r = p2s.at[k, a], p2r.at[k, a]
-        landed(x2.at[k, a, 0, 1], s.at[0], r.at[0])
-        landed(x2.at[k, a, 1, 0], s.at[1], r.at[1])
-        landed(x2.at[k, a, 0, 0], s.at[2], r.at[2])
-        landed(x2.at[k, a, 1, 1], s.at[3], r.at[3])
+        landed(x2.at[k, a], s.at[0], r.at[0])
         for half in range(2):
             own = rows_of(k, a, OWN, half * 4)[...].astype(F32)
             both = x2[k, a, 0, half].astype(F32) + x2[k, a, 1, half].astype(F32)
             xsum[k, a, half] = (own + both).astype(BF16)
         s, r = t1s.at[k, a], t1r.at[k, a]
         for o in range(1, 4):
-            send(xsum.at[k, a, :, (zi + o) % 4], zr1.at[k, a, o - 1], s.at[o - 1], r.at[o - 1],
+            send(xsum.at[k, a, :, (zi + o) % 4], zr1.at[k, a, o - 1], s.at[o - 1], r.at[0],
                  mates[o])
 
     def sum_fourth(k, a):
-        for o in range(3):
-            landed(zr1.at[k, a, o], t1s.at[k, a, o], t1r.at[k, a, o])
+        landed(zr1.at[k, a], t1s.at[k, a], t1r.at[k, a, 0])
 
         def quad_sum(quad):
             acc = xsum[k, a, quad, zi].astype(F32)
@@ -331,13 +337,11 @@
         landed(n_at(g, PREV, other, o), s.at[0], r.at[0])
         push(n_at(g, PREV, other, o).at[:, :half], s, r, 2, x_up)
         landed(n_at(g, NEXT, other, o), s.at[1], r.at[1])
-        push(n_at(g, NEXT, other, o).at[:, half:], s, r, 3, x_dn)
+        push(n_at(g, NEXT, other, o).at[:, half:], s, r, 2, x_dn)
 
     def gx_last(g, other, o):
         s, r = gxs.at[g, other, o], gxr.at[g, other, o]
-        half = nb[g].shape[-1] // 2
-        landed(n_at(g, FAR, other, o).at[:, :half], s.at[2], r.at[2])
-        landed(n_at(g, FAR, other, o).at[:, half:], s.at[3], r.at[3])
+        landed(n_at(g, FAR, other, o), s.at[2], r.at[2])
 
     def gz_landed(g, other, o):
         landed(n_at(g, OWN, other, o), gzs.at[g, other, o], gzr.at[g, other, o])
@@ -347,13 +351,13 @@
         mine = n_at(g, OWN, 0, 0)
         send(mine, mine, gzs.at[g, 1, 0], gzr.at[g, 1, 0], across)
         for o in (1, 3, 2):
-            push(mine, gzs.at[g, 0], gzr.at[g, 0], o, mates[o])
+            push(mine, gzs.at[g, 0, o], gzr.at[g, 0], o, mates[o])
         gx_start(g, 0, 0)
 
     def g_across(g):
         gz_landed(g, 1, 0)
         for o in (1, 3, 2):
-            push(n_at(g, OWN, 1, 0), gzs.at[g, 1], gzr.at[g, 1], o, mates[o])
+            push(n_at(g, OWN, 1, 0), gzs.at[g, 1, o], gzr.at[g, 1], o, mates[o])
 
     def g_quad(g, other):
         for o in (1, 3, 2):
@@ -410,10 +414,11 @@
     gain[...] = gain_ref[...].astype(F32).reshape(1, -1)
     oy_third(OWN, 0)
     oy_third(OWN, 1)
-    q_first()
+    far = q_first()
     qy_up(PREV)
     qy_dn(NEXT)
     q_second()
+    left(*far)
     o_start(0)
     qy_dn(PREV)
     qy_up(NEXT)
@@ -519,9 +524,9 @@
     g_quad(1, 1)
     g_ring(2, 0)
     g_quad(2, 1)
+    put(OWN)
     g_ring(1, 1)
     g_ring(2, 1)
-    put(OWN)
     put(PREV)
     put(NEXT)
     for g in range(3):
@@ -529,8 +534,12 @@
             for o in (0, 1, 3, 2):
                 gx_last(g, other, o)
     put(FAR)
-    for copy in sent:
-        copy.wait_send()
+    all_sent = [
+        (wq.at[:29], 0), (wo.at[:31], 5), (part.at[:3], 6), (zr1, 7), (zr2, 8),
+        *((rows.at[:31], 9 + g) for g, rows in enumerate(nb)),
+    ]
+    for ref, i in all_sent:
+        remote(ref, ref, left_sem.at[i], zqr.at[0], sib).wait_send()
     for copy in outs:
         copy.wait()
 
@@ -554,7 +563,6 @@
     dma, vmem = pltpu.SemaphoreType.DMA, pltpu.VMEM
     any_spec = pl.BlockSpec(memory_space=pl.ANY)
     vmem_spec = pl.BlockSpec(memory_space=pltpu.VMEM)
-    twice = lambda *shape: [dma(shape), dma(shape)]
     return pl.pallas_call(
         block_kernel,
         name="block",
@@ -590,10 +598,11 @@
             vmem((own_count, width), BF16),
             vmem((1, width), F32),
             dma((8,)), dma((5,)),
-            *twice(6), *twice(4, 6), *twice(4, 4),
-            *twice(8), *twice(4, 2, 4), *twice(4, 2, 4),
-            *twice(4, 2, 2), *twice(4, 2, 4), *twice(4, 2, 3), *twice(4, 2),
-            *twice(3, 2, 4), *twice(3, 2, 4, 4),
+            dma((12,)),
+            dma((6,)), dma((4, 6)), dma((4, 4)),
+            dma((8,)), dma((4, 2, 4)), dma((4, 2, 4)),
+            dma((4, 2, 2)), dma((4, 2, 1)), dma((4, 2, 1)), dma((4, 2)),
+            dma((3, 2, 4)), dma((3, 2, 4, 3)),
         ],
         compiler_params=pltpu.CompilerParams(
             collective_id=0, has_side_effects=True, vmem_limit_bytes=67043328

time: 170 us -> 167 us (0.982)
  Pallas kernels: 165 us -> 162 us
    pallas_call x1, Pallas kernels: 165 us -> 162 us  [body(): pl.pallas_call(block_kernel, name='block', out_shape=(jax.ShapeDtypeStruc...]
where the time goes in v3:
time: 167 us
  Pallas kernels  162 us (97%)
  local copies, waits for them, and re-layouts  4.59 us (3%)
    pallas_call x1, Pallas kernels, body(): pl.pallas_call(block_kernel, name='block', out_shape=(jax.ShapeDtypeStruc...  162 us
    unnamed x2, local copies, waits for them, and re-layouts  4.59 us

profile of v3, /device:TPU:32, one launch (start us, length us, event | category | flops | bytes accessed | tf_op | source)
XLA Modules:
  0.0 167.0 jit_solution(1753426740501837685)
XLA Ops:
  0.6 161.8 %block.1 = (bf16[4,8192]{1,0:T(4,128)(2,1)}, bf16[128,8192]{1,0:T(8,128)(2,1)}) custom-call(bf16[128,8192]{1,0:T(8,128)(2,1)} %x_hbm.1, bf16[2,128,256]{2,1,0:T(8,128)(2,1)} %bitcast.6, bf16[2,128,256]{2,1,0:T(8,128)(2,1)} %bitcast.7, bf16[1024,128]{1,0:T(8,128)(2,1)} %bitcast.4, bf16[1024,128]{1,0:T(8,128)(2,1)} %bitcast.5, ...), custom_call_target="tpu_custom_call" | custom-call | tf_op jit(solution)/shard_map/block/pallas_call | solution.py:566
  162.4 1.5 copy.13
  163.9 3.1 %copy.14 = bf16[128,8192]{1,0:T(8,128)(2,1)} copy(bf16[128,8192]{1,0:T(8,128)(2,1)} %get-tuple-element.5) | data formatting | bytes 4194304
